TPU v7x, 128 devices: a 2x2x16 block of a 8x8x16 slice. The times are simulated.
128 devices in a mesh: groups: 4 (over x, y), seq: 32 (over z, core).
Axes of the slice: x: 2, y: 2, z: 16, core: 2. Of those that a mesh axis runs over, the one named last changes fastest.
The devices are a block of a 8x8x16 slice.
Arguments:
- queries: bfloat16 [8192, 24576], P(('groups', 'seq')), parts along dimension 0, may hold values from -500 to 500
- kv_new: bfloat16 [8192, 576], P(('groups', 'seq')), parts along dimension 0, may hold values from -6 to 6
- kv_cache: bfloat16 [4096, 576], P(('groups', 'seq')), parts along dimension 0, may hold values from -6 to 6
- kv_gain: float32 [512], replicated, may hold values from 0.5 to 2
- w_key: bfloat16 [512, 16384], P(None, 'seq'), may hold values from -0.25 to 0.25
- w_value: bfloat16 [512, 16384], P(None, 'seq'), may hold values from -0.25 to 0.25
- prefix_len: int32 [4], P('groups'), parts along dimension 0, may hold values from 256 to 1024
Outputs:
- attended: bfloat16 [8192, 16384], P(('groups', 'seq')), parts along dimension 0
There are 4 independent parts, one for each index of `groups`. A program takes and returns all parts, laid end to end along the dimension named above; an argument that names none is the same for every part. Nothing has to cross between parts.
Inputs may be any that keep to these rules, and one draw needn't show every extreme that they name: The stretch's tokens take positions from prefix_len on.
All inputs are finite; a program needn't handle non-finite values.
Results may differ from a plain program's by a relative error of at most 0.012.
Values may be sent and summed in bfloat16 or wider, within the bound.
A program may use at most 128 MiB of HBM per device.

v0:
```python
import math

import jax
import jax.numpy as jnp
from jax import lax
from jax.sharding import Mesh
from jax.sharding import PartitionSpec as P

NOPE = 128
ROPE = 64
LATENT = 512
VH = 128
SEQ = ("seq_0", "seq_1")
GROUPS_SEQ = ("groups", "seq_0", "seq_1")


epsilon = 1e-06


def cut_along(array, dim, peers):
    before, after = (array.shape[:dim], array.shape[dim + 1 :])
    return jnp.moveaxis(array.reshape(*before, peers, -1, *after), dim, 0)


def laid_out(parts, dim):
    parts = jnp.moveaxis(parts, 0, dim)
    dims = parts.shape
    return parts.reshape(*dims[:dim], dims[dim] * dims[dim + 1], *dims[dim + 2 :])


def turned_blocks(parts, axes, turns):
    dims = [lax.axis_size(a) for a in axes]
    parts = parts.reshape(*dims, *parts.shape[1:])
    for k in turns:
        parts = lax.all_to_all(parts, axes[k], split_axis=k, concat_axis=k, tiled=True)
    return parts.reshape(-1, *parts.shape[len(axes) :])


def exchange_by_chip(array, groups, turns, split_dim, concat_dim):
    peers = lax.axis_size(groups[0]) * lax.axis_size(groups[1])
    parts = cut_along(array, split_dim, peers)
    return laid_out(turned_blocks(parts, groups, turns), concat_dim)


def phases_for(positions, rope_width):
    half_width = rope_width // 2
    inverse = 10000.0 ** (-(jnp.arange(half_width, dtype=jnp.float32) * 2.0) / rope_width)
    return positions.astype(jnp.float32)[:, None] * inverse[None, :]


def rotate(values, phases):
    half_width = values.shape[-1] // 2
    front_half = values[..., :half_width]
    back_half = values[..., half_width:]
    cosine = jnp.cos(phases)
    sine_part = jnp.sin(phases)
    return jnp.concatenate(
        [front_half * cosine - back_half * sine_part, back_half * cosine + front_half * sine_part],
        -1,
    )


def local(queries, kv_new, kv_cache, kv_gain, w_key, w_value, prefix_len):
    groups_seq = lax.axis_size(SEQ)
    my_rank = lax.axis_index(SEQ)
    tok_dev = queries.shape[0]
    cache_dev = kv_cache.shape[0]
    heads_dev = w_key.shape[1] // NOPE
    heads_all = heads_dev * groups_seq
    stretch_start = prefix_len[0]
    positions = stretch_start + my_rank * tok_dev + jnp.arange(tok_dev, dtype=jnp.int32)
    phases = phases_for(positions, ROPE)
    raw_latent = kv_new[:, :LATENT].astype(jnp.float32)
    inv_rms = lax.rsqrt(jnp.mean(raw_latent * raw_latent, axis=1, keepdims=True) + epsilon)
    latent_new = (raw_latent * inv_rms * kv_gain[None, :]).astype(jnp.bfloat16)
    rope_new = rotate(kv_new[:, LATENT:].astype(jnp.float32), phases).astype(jnp.bfloat16)
    new_rows = jnp.concatenate([latent_new, rope_new], 1)
    gathered = lax.all_gather(jnp.concatenate([kv_cache, new_rows], 0), SEQ, axis=0, tiled=True)
    stacked = gathered.reshape(groups_seq, cache_dev + tok_dev, LATENT + ROPE)
    keys_all = jnp.concatenate(
        [
            stacked[:, :cache_dev].reshape(-1, LATENT + ROPE),
            stacked[:, cache_dev:].reshape(-1, LATENT + ROPE),
        ],
        0,
    )
    query_heads = queries.reshape(tok_dev, heads_all, NOPE + ROPE)
    query_rot = rotate(query_heads[:, :, NOPE:].astype(jnp.float32), phases[:, None, :]).astype(
        jnp.bfloat16
    )
    query_ready = jnp.concatenate([query_heads[:, :, :NOPE], query_rot], 2).reshape(
        tok_dev, heads_all * (NOPE + ROPE)
    )
    query_local = lax.all_to_all(query_ready, SEQ, split_axis=1, concat_axis=0, tiled=True)
    tokens_all = groups_seq * tok_dev
    cached_all = groups_seq * cache_dev
    query_local = query_local.reshape(tokens_all, heads_dev, NOPE + ROPE)
    latent_all = keys_all[:, :LATENT]
    key_rope = keys_all[:, LATENT:]
    key_nope = (
        jnp.dot(latent_all, w_key, preferred_element_type=jnp.float32)
        .astype(jnp.bfloat16)
        .reshape(-1, heads_dev, NOPE)
    )
    value_rows = (
        jnp.dot(latent_all, w_value, preferred_element_type=jnp.float32)
        .astype(jnp.bfloat16)
        .reshape(-1, heads_dev, VH)
    )
    block_rows = min(512, tokens_all)
    score_scale = 1.0 / math.sqrt(NOPE + ROPE)
    pieces = []
    for block_index in range(tokens_all // block_rows):
        row_first = block_index * block_rows
        new_count = row_first + block_rows
        span_keys = cached_all + new_count
        query_block = query_local[row_first : row_first + block_rows]
        scores = jnp.einsum(
            "thd,shd->hts",
            query_block[:, :, :NOPE],
            key_nope[:span_keys],
            preferred_element_type=jnp.float32,
        )
        scores = scores + jnp.einsum(
            "thr,sr->hts",
            query_block[:, :, NOPE:],
            key_rope[:span_keys],
            preferred_element_type=jnp.float32,
        )
        key_index = jnp.arange(span_keys, dtype=jnp.int32)[None, :]
        row_index = row_first + jnp.arange(block_rows, dtype=jnp.int32)[:, None]
        live_mask = jnp.where(
            key_index < cached_all, key_index < stretch_start, key_index - cached_all <= row_index
        )
        scores = jnp.where(live_mask[None], scores * score_scale, -1e30)
        top_score = jnp.max(scores, axis=2, keepdims=True)
        exp_scores = jnp.exp(scores - top_score)
        weights = (exp_scores / jnp.sum(exp_scores, axis=2, keepdims=True)).astype(jnp.bfloat16)
        mixed_out = jnp.einsum(
            "hts,shd->thd", weights, value_rows[:span_keys], preferred_element_type=jnp.float32
        )
        pieces.append(mixed_out.astype(jnp.bfloat16).reshape(block_rows, heads_dev * VH))
    attended = jnp.concatenate(pieces, 0)
    result_rows = exchange_by_chip(attended, ("seq_0", "seq_1"), (1, 0), 0, 1)
    return result_rows


def solution(mesh):
    torus = Mesh(mesh.devices.reshape(mesh.shape["groups"], 16, 2), ("groups", "seq_0", "seq_1"))
    placed = (
        P(GROUPS_SEQ, None),
        P(GROUPS_SEQ, None),
        P(GROUPS_SEQ, None),
        P(),
        P(None, SEQ),
        P(None, SEQ),
        P("groups"),
    )
    return jax.shard_map(
        local, mesh=torus, in_specs=placed, out_specs=P(GROUPS_SEQ, None), check_vma=False
    )
```

profile of v0, /device:TPU:86, one launch (start us, length us, event | category | flops | bytes accessed | tf_op | source)
XLA Modules:
  0.0 574.3 jit_solution(15806090265100492507)
XLA Ops:
  6.6 7.4 %reshape.426 = bf16[64,128,192]{2,1,0:T(8,128)(2,1)} reshape(bf16[64,24576]{1,0:T(8,128)(2,1)} %param.7) | data formatting | bytes 6291456 | tf_op jit(solution)/shard_map/reshape | solution.py:87
  13.9 4.1 slice_convert_fusion
  18.8 0.2 multiply_cosine_fusion
  19.0 5.1 subtract_convert_fusion
  24.1 3.4 pad_maximum_fusion
  27.5 8.0 %all_to_all.18 = bf16[64,32,768]{2,1,0:T(8,128)(2,1)} reshape(bf16[64,128,192]{2,1,0:T(8,128)(2,1)} %pad_maximum_fusion) | data formatting | bytes 6291456 | tf_op jit(solution)/shard_map/all_to_all | solution.py:94
  35.6 5.3 copy.101
  40.9 17.9 %all-to-all-start = ((bf16[64,32,768]{2,0,1:T(8,128)(2,1)}), bf16[64,32,768]{2,0,1:T(8,128)(2,1)}, u32[]{:S(2)}, u32[]{:S(2)}) async-start(bf16[64,32,768]{2,0,1:T(8,128)(2,1)} %copy.101), calls=%async_computation | async-start | bytes 6291456 | tf_op jit(solution)/shard_map/all_to_all | solution.py:94
  58.8 0.2 all-gather.2.cloned.1.call-start
  59.1 0.1 fusion.46
  59.2 0.1 fusion.48
  59.3 0.7 maximum_maximum_fusion
  60.1 0.1 all-gather.2.cloned.1.call-update
  60.3 1.4 fusion.17
  61.7 1.8 compare_select_fusion.2
  63.5 2.1 compare_select_fusion.1
  65.6 2.3 compare_select_fusion
  67.9 132.5 %all-gather.2.cloned.1.call-done = bf16[3072,576]{1,0:T(8,128)(2,1)} async-done(((bf16[96,576]{1,0:T(8,128)(2,1)}), bf16[3072,576]{1,0:T(8,128)(2,1)}) %all-gather.2.cloned.1.call-update) | async-done | bytes 3538960 | tf_op jit(solution)/shard_map/all_gather | solution.py:78
  200.4 3.5 slice.178
  203.9 2.5 slice.177
  206.4 2.9 copy.100
  209.3 2.4 copy.99
  211.7 3.1 convolution_convert_fusion
  214.8 0.0 copy-start.13
  214.8 2.1 copy-done.2
  217.0 0.4 copy-done.13
  217.4 2.2 convolution_convert_fusion.1
  219.5 1.4 slice.181
  220.9 1.5 slice.192
  222.4 1.7 slice.202
  224.1 1.7 slice.199
  225.8 3.6 fusion.59
  229.4 3.4 slice.146
  232.9 3.4 slice.155
  236.3 3.5 slice.164
  239.8 3.8 slice.171
  243.6 0.0 slice-start.4
  243.6 2.8 fusion.31
  246.5 6.2 %fusion.11 = f32[4,512,1536]{2,1,0:T(8,128)} fusion(f32[1536,512,4]{0,1,2:T(8,128)S(1)} %fusion.31, bf16[1536,4,128]{0,2,1:T(8,128)(2,1)S(1)} %bitcast.91, pred[512,1536]{1,0:T(8,128)(4,1)S(1)} %copy-done.6, bf16[512,4,128]{2,1,0:T(4,128)(2,1)S(1)} %slice-done.4), kind=kOutput, calls=%fused_computation.21 | convolution fusion | flops 814743552 | bytes 28049408 | tf_op jit(solution)/shard_map/thd,shd->hts/dot_general | solution.py:118
  252.7 10.4 %fusion.63 = f32[4,512]{1,0:T(4,128)S(1)} fusion(f32[4,512,1536]{2,1,0:T(8,128)} %fusion.11), kind=kOutput, calls=%fused_computation.115 | output fusion | flops 6292991 | bytes 12591104 | tf_op jit(solution)/shard_map/sub | solution.py:137
  263.1 10.9 %fusion.18 = bf16[4,128,512]{2,1,0:T(8,128)(2,1)S(1)} fusion(bf16[1536,4,128]{0,2,1:T(8,128)(2,1)} %bitcast.103, f32[4,512]{1,0:T(4,128)S(1)} %fusion.63, f32[4,512,1536]{2,1,0:T(8,128)} %fusion.11), kind=kOutput, calls=%fused_computation.49 | convolution fusion | flops 815009280 | bytes 14688256 | tf_op jit(solution)/shard_map/hts,shd->thd/dot_general | solution.py:139
  274.1 1.0 copy.118
  275.1 9.1 %fusion.28 = f32[2048,512,4]{0,1,2:T(8,128)} fusion(bf16[512,4,64]{2,1,0:T(4,128)(2,1)S(1)} %slice-done.5, bf16[2048,576]{0,1:T(8,128)(2,1)S(1)} %copy.100, bf16[1024,576]{0,1:T(8,128)(2,1)} %copy.99), kind=kOutput, calls=%fused_computation.59 | convolution fusion | flops 537395200 | bytes 20578304 | tf_op jit(solution)/shard_map/thr,sr->hts/dot_general | solution.py:124
  284.2 11.4 %fusion.9 = f32[4,512,2048]{2,1,0:T(8,128)} fusion(f32[2048,512,4]{0,1,2:T(8,128)} %fusion.28, pred[512,2048]{1,0:T(8,128)(4,1)S(1)} %copy-done.5, bf16[2048,4,128]{0,2,1:T(8,128)(2,1)S(1)} %bitcast.92, bf16[512,4,128]{2,1,0:T(4,128)(2,1)S(1)} %slice-done.6), kind=kOutput, calls=%fused_computation.16 | convolution fusion | flops 1086324736 | bytes 37224448 | tf_op jit(solution)/shard_map/thd,shd->hts/dot_general | solution.py:118
  295.6 13.3 %fusion.62 = f32[4,512]{1,0:T(4,128)S(1)} fusion(f32[4,512,2048]{2,1,0:T(8,128)} %fusion.9), kind=kOutput, calls=%fused_computation.114 | output fusion | flops 8390655 | bytes 16785408 | tf_op jit(solution)/shard_map/sub | solution.py:137
  308.9 13.6 %fusion.19 = bf16[4,128,512]{2,1,0:T(8,128)(2,1)S(1)} fusion(bf16[2048,4,128]{0,2,1:T(8,128)(2,1)} %bitcast.102, f32[4,512]{1,0:T(4,128)S(1)} %fusion.62, f32[4,512,2048]{2,1,0:T(8,128)} %fusion.9), kind=kOutput, calls=%fused_computation.50 | convolution fusion | flops 1086590976 | bytes 19406848 | tf_op jit(solution)/shard_map/hts,shd->thd/dot_general | solution.py:139
  322.5 1.0 copy.119
  323.5 9.5 %fusion.25 = f32[2560,512,4]{0,1,2:T(8,128)} fusion(bf16[512,4,64]{2,1,0:T(4,128)(2,1)S(1)} %slice-done.7, bf16[2048,576]{0,1:T(8,128)(2,1)S(1)} %copy.100, bf16[1024,576]{0,1:T(8,128)(2,1)} %copy.99), kind=kOutput, calls=%fused_computation.56 | convolution fusion | flops 671744000 | bytes 24772608 | tf_op jit(solution)/shard_map/thr,sr->hts/dot_general | solution.py:124
  333.0 14.5 %fusion.7 = f32[4,512,2560]{2,1,0:T(8,128)} fusion(f32[2560,512,4]{0,1,2:T(8,128)} %fusion.25, pred[512,2560]{1,0:T(8,128)(4,1)} %compare_select_fusion.1, bf16[2560,4,128]{0,2,1:T(8,128)(2,1)} %bitcast.93, bf16[512,4,128]{2,1,0:T(4,128)(2,1)S(1)} %slice-done.8), kind=kOutput, calls=%fused_computation.11 | convolution fusion | flops 1357905920 | bytes 46399488 | tf_op jit(solution)/shard_map/thd,shd->hts/dot_general | solution.py:118
  347.6 16.8 %fusion.61 = f32[4,512]{1,0:T(4,128)S(1)} fusion(f32[4,512,2560]{2,1,0:T(8,128)} %fusion.7), kind=kOutput, calls=%fused_computation.113 | output fusion | flops 10488319 | bytes 20979712 | tf_op jit(solution)/shard_map/sub | solution.py:137
  364.3 16.5 %fusion.20 = bf16[4,128,512]{2,1,0:T(8,128)(2,1)S(1)} fusion(bf16[2560,4,128]{0,2,1:T(8,128)(2,1)} %bitcast.101, f32[4,512]{1,0:T(4,128)S(1)} %fusion.61, f32[4,512,2560]{2,1,0:T(8,128)} %fusion.7), kind=kOutput, calls=%fused_computation.51 | convolution fusion | flops 1358172672 | bytes 24125440 | tf_op jit(solution)/shard_map/hts,shd->thd/dot_general | solution.py:139
  380.9 1.0 copy.120
  381.9 11.0 %fusion.22 = f32[3072,512,4]{0,1,2:T(8,128)} fusion(bf16[512,4,64]{2,1,0:T(4,128)(2,1)S(1)} %slice-done.9, bf16[2048,576]{0,1:T(8,128)(2,1)S(1)} %copy.100, bf16[1024,576]{0,1:T(8,128)(2,1)} %copy.99), kind=kOutput, calls=%fused_computation.53 | convolution fusion | flops 806092800 | bytes 28966912 | tf_op jit(solution)/shard_map/thr,sr->hts/dot_general | solution.py:124
  392.8 17.1 %fusion.5 = f32[4,512,3072]{2,1,0:T(8,128)} fusion(f32[3072,512,4]{0,1,2:T(8,128)} %fusion.22, pred[512,3072]{1,0:T(8,128)(4,1)} %compare_select_fusion, bf16[3072,4,128]{0,2,1:T(8,128)(2,1)} %bitcast.90, bf16[512,4,128]{2,1,0:T(4,128)(2,1)S(1)} %slice-done.10), kind=kOutput, calls=%fused_computation.6 | convolution fusion | flops 1629487104 | bytes 55574528 | tf_op jit(solution)/shard_map/thd,shd->hts/dot_general | solution.py:118
  410.0 19.6 %fusion.60 = f32[4,512]{1,0:T(4,128)S(1)} fusion(f32[4,512,3072]{2,1,0:T(8,128)} %fusion.5), kind=kOutput, calls=%fused_computation.112 | output fusion | flops 12585983 | bytes 25174016 | tf_op jit(solution)/shard_map/sub | solution.py:137
  429.6 0.0 copy-start.9
  429.6 18.3 %fusion.21 = bf16[4,128,512]{2,1,0:T(8,128)(2,1)S(1)} fusion(bf16[3072,4,128]{0,2,1:T(8,128)(2,1)} %bitcast.94, f32[4,512]{1,0:T(4,128)S(1)} %fusion.60, f32[4,512,3072]{2,1,0:T(8,128)} %fusion.5), kind=kOutput, calls=%fused_computation.52 | convolution fusion | flops 1629754368 | bytes 28844032 | tf_op jit(solution)/shard_map/hts,shd->thd/dot_general | solution.py:139
  448.0 0.2 copy.121
  448.2 0.1 pad_maximum_fusion.1
  448.4 0.2 copy.122
  448.6 5.4 all_to_all.26
  454.0 0.2 copy.123
  454.3 111.5 %all_to_all.27 = bf16[16,2,64,512]{3,2,1,0:T(8,128)(2,1)S(1)} all-to-all(bf16[16,2,64,512]{3,2,1,0:T(8,128)(2,1)S(1)} %copy.123), channel_id=1, replica_groups=mesh['groups'=4,'seq_0'=16,'seq_1'=2] {'seq_0'}, dimensions={0} | all-to-all | bytes 4194304 | tf_op jit(solution)/shard_map/all_to_all | solution.py:35
  565.7 1.5 copy.141
  (61 shorter events, 0.2 us)
Async XLA Ops:
  6.5 205.2 %copy-start = (bf16[512,512]{1,0:T(8,128)(2,1)S(1)}, bf16[512,512]{1,0:T(8,128)(2,1)}, u32[]{:S(2)}) copy-start(bf16[512,512]{1,0:T(8,128)(2,1)} %param.11) | copy-start | bytes 1572868
  13.9 4.8 copy-start.10
  19.0 5.1 slice-start.2
  40.9 18.3 %copy-start.12 = (f32[512]{0:T(512)S(1)}, f32[512]{0:T(512)}, u32[]{:S(2)}) copy-start(f32[512]{0:T(512)} %param.10) | copy-start | bytes 6148
  40.9 18.4 %copy-start.11 = (bf16[32,576]{1,0:T(8,128)(2,1)S(1)}, bf16[32,576]{1,0:T(8,128)(2,1)}, u32[]{:S(2)}) copy-start(bf16[32,576]{1,0:T(8,128)(2,1)} %param.9) | copy-start | bytes 110596
  40.9 184.9 %all-to-all-start = ((bf16[64,32,768]{2,0,1:T(8,128)(2,1)}), bf16[64,32,768]{2,0,1:T(8,128)(2,1)}, u32[]{:S(2)}, u32[]{:S(2)}) async-start(bf16[64,32,768]{2,0,1:T(8,128)(2,1)} %copy.101), calls=%async_computation | async-start | bytes 6291456 | tf_op jit(solution)/shard_map/all_to_all | solution.py:94
  58.8 141.5 %all-gather.2.cloned.1.call-start = ((), (), s32[]{:S(2)}) async-start(), calls=%async_computation.3 | async-start | bytes 4055040 | tf_op jit(solution)/shard_map/all_gather | solution.py:78
  214.8 7.6 %copy-start.3 = (bf16[3072,512]{0,1:T(8,128)(2,1)}, bf16[3072,512]{0,1:T(8,128)(2,1)S(1)}, u32[]{:S(2)}) copy-start(bf16[3072,512]{0,1:T(8,128)(2,1)S(1)} %convolution_convert_fusion) | copy-start | bytes 9437188
  214.8 2.1 copy-start.2
  214.8 2.5 copy-start.13
  219.5 4.5 copy-start.4
  236.3 7.3 %slice-start.3 = ((bf16[512,4,192]{2,1,0:T(4,128)(2,1)}), bf16[512,4,64]{2,1,0:T(4,128)(2,1)S(1)}, s32[]{:S(2)}) async-start(bf16[512,4,192]{2,1,0:T(4,128)(2,1)} %slice.146), calls=%async_computation.7 | async-start | bytes 1048576 | tf_op jit(solution)/shard_map/slice | solution.py:126
  243.6 2.9 slice-start
  243.6 2.9 slice-start.4
  243.6 2.9 copy-start.6
  263.1 12.0 %slice-start.5 = ((bf16[512,4,192]{2,1,0:T(4,128)(2,1)}), bf16[512,4,64]{2,1,0:T(4,128)(2,1)S(1)}, s32[]{:S(2)}) async-start(bf16[512,4,192]{2,1,0:T(4,128)(2,1)} %slice.155), calls=%async_computation.9 | async-start | bytes 1048576 | tf_op jit(solution)/shard_map/slice | solution.py:126
  275.1 9.1 %slice-start.1 = ((bf16[3072,512]{0,1:T(8,128)(2,1)}), bf16[2048,512]{0,1:T(8,128)(2,1)S(1)}, s32[]{:S(2)}) async-start(bf16[3072,512]{0,1:T(8,128)(2,1)} %copy-done.3), calls=%async_computation.5 | async-start | bytes 4194304 | tf_op jit(solution)/shard_map/slice | solution.py:121
  275.1 9.1 %copy-start.5 = (pred[512,2048]{1,0:T(8,128)(4,1)S(1)}, pred[512,2048]{1,0:T(8,128)(4,1)}, u32[]{:S(2)}) copy-start(pred[512,2048]{1,0:T(8,128)(4,1)} %compare_select_fusion.2) | copy-start | bytes 3145732
  275.1 9.1 %slice-start.6 = ((bf16[512,4,192]{2,1,0:T(4,128)(2,1)}), bf16[512,4,128]{2,1,0:T(4,128)(2,1)S(1)}, s32[]{:S(2)}) async-start(bf16[512,4,192]{2,1,0:T(4,128)(2,1)} %slice.155), calls=%async_computation.10 | async-start | bytes 1048576 | tf_op jit(solution)/shard_map/slice | solution.py:120
  308.9 14.7 %slice-start.7 = ((bf16[512,4,192]{2,1,0:T(4,128)(2,1)}), bf16[512,4,64]{2,1,0:T(4,128)(2,1)S(1)}, s32[]{:S(2)}) async-start(bf16[512,4,192]{2,1,0:T(4,128)(2,1)} %slice.164), calls=%async_computation.11 | async-start | bytes 1048576 | tf_op jit(solution)/shard_map/slice | solution.py:126
  323.5 9.5 %slice-start.8 = ((bf16[512,4,192]{2,1,0:T(4,128)(2,1)}), bf16[512,4,128]{2,1,0:T(4,128)(2,1)S(1)}, s32[]{:S(2)}) async-start(bf16[512,4,192]{2,1,0:T(4,128)(2,1)} %slice.164), calls=%async_computation.12 | async-start | bytes 1048576 | tf_op jit(solution)/shard_map/slice | solution.py:120
  364.3 17.5 %slice-start.9 = ((bf16[512,4,192]{2,1,0:T(4,128)(2,1)}), bf16[512,4,64]{2,1,0:T(4,128)(2,1)S(1)}, s32[]{:S(2)}) async-start(bf16[512,4,192]{2,1,0:T(4,128)(2,1)} %slice.171), calls=%async_computation.13 | async-start | bytes 1048576 | tf_op jit(solution)/shard_map/slice | solution.py:126
  381.9 11.0 %slice-start.10 = ((bf16[512,4,192]{2,1,0:T(4,128)(2,1)}), bf16[512,4,128]{2,1,0:T(4,128)(2,1)S(1)}, s32[]{:S(2)}) async-start(bf16[512,4,192]{2,1,0:T(4,128)(2,1)} %slice.171), calls=%async_computation.14 | async-start | bytes 1048576 | tf_op jit(solution)/shard_map/slice | solution.py:120
  429.6 18.6 %copy-start.7 = (bf16[512,512]{1,0:T(8,128)(2,1)S(1)}, bf16[512,512]{1,0:T(8,128)(2,1)}, u32[]{:S(2)}) copy-start(bf16[512,512]{1,0:T(8,128)(2,1)} %copy.118) | copy-start | bytes 1572868
  429.6 18.6 %copy-start.8 = (bf16[512,512]{1,0:T(8,128)(2,1)S(1)}, bf16[512,512]{1,0:T(8,128)(2,1)}, u32[]{:S(2)}) copy-start(bf16[512,512]{1,0:T(8,128)(2,1)} %copy.119) | copy-start | bytes 1572868
  429.6 18.6 %copy-start.9 = (bf16[512,512]{1,0:T(8,128)(2,1)S(1)}, bf16[512,512]{1,0:T(8,128)(2,1)}, u32[]{:S(2)}) copy-start(bf16[512,512]{1,0:T(8,128)(2,1)} %copy.120) | copy-start | bytes 1572868
  454.0 113.2 %copy-start.1 = (bf16[512,512]{1,0:T(8,128)(2,1)S(1)}, bf16[512,512]{1,0:T(8,128)(2,1)}, u32[]{:S(2)}) copy-start(bf16[512,512]{1,0:T(8,128)(2,1)} %param.11) | copy-start | bytes 1572868
Sparse Core Ops, SparseCore 0:
  61.4 138.9 all-gather.1
where the time goes:
time: 582 us; the launch traced here: 574 us
  matrix products  146 us (25%)
  waiting for transfers between devices  133 us (23%)
  blocking collectives  117 us (20%)
  other arithmetic  81.8 us (14%)
  local copies, waits for them, and re-layouts  63.9 us (11%)
  starting transfers between devices  18.2 us (3%)
  between operations  14.8 us (3%)
    all_gather x1, waiting for transfers between devices, local(): lax.all_gather(jnp.concatenate([kv_cache, new_rows], 0), SEQ, axis=0, til...  132 us
    all_to_all x2, blocking collectives, turned_blocks(): lax.all_to_all(parts, axes[k], split_axis=k, concat_axis=k, tiled=True)  117 us
    sub x4, other arithmetic, local(): exp_scores = jnp.exp(scores - top_score)  60.1 us
    dot_general x4, matrix products, local(): jnp.einsum('hts,shd->thd', weights, value_rows[:span_keys], preferred_ele...  59.5 us
    dot_general x4, matrix products, local(): jnp.einsum('thd,shd->hts', query_block[:, :, :NOPE], key_nope[:span_keys]...  49.2 us
    dot_general x4, matrix products, local(): jnp.einsum('thr,sr->hts', query_block[:, :, NOPE:], key_rope[:span_keys],...  32.4 us
    all_to_all x1, starting transfers between devices, local(): lax.all_to_all(query_ready, SEQ, split_axis=1, concat_axis=0, tiled=True)  17.9 us
    slice x5, local copies, waits for them, and re-layouts, local(): query_block = query_local[row_first:row_first + block_rows]  17.8 us
  transfers between devices with their start and end apart: 2, of which 1 were waited for; matrix products, arithmetic and copies ran while one was open for 5% of the time, Pallas kernels for 0%

commit v1 on v0

v1 whole, which is shorter than its diff:
```python
import functools
import math

import jax
import jax.numpy as jnp
from jax import lax
from jax.experimental import pallas as pl
from jax.experimental.pallas import tpu as pltpu
from jax.sharding import Mesh
from jax.sharding import PartitionSpec as P

NOPE = 128
ROPE = 64
LATENT = 512
VH = 128
WIDE = 640
BLOCK = 512
AXES = ("gx", "px", "gy", "py", "z", "c")
GROUPS = ("gx", "px", "gy", "py")
SEQ = ("z", "c")
EPSILON = 1e-06
DEAD = -1e30
MESH = pl.DeviceIdType.MESH
NT = (((1,), (1,)), ((), ()))


def kernel(
    dims,
    q_hbm,
    rows_hbm,
    wk_hbm,
    wv_hbm,
    turn_ref,
    out_ref,
    w,
    keys,
    q,
    qs,
    scores,
    acc,
    top,
    total,
    local_sem,
    kr_s,
    kr_r,
    kc_s,
    kc_r,
    wr_s,
    wr_r,
    wx_s,
    wx_r,
    wc_s,
    wc_r,
):
    ring, tok, cache, heads = dims
    far = ring // 2
    z = lax.axis_index("z")
    c = lax.axis_index("c")
    px = lax.axis_index("px")
    py = lax.axis_index("py")
    rank = z * 2 + c
    cached_all = ring * 2 * cache
    half_rows = LATENT // 2
    up = {"z": lax.rem(z + 1, ring)}
    down = {"z": lax.rem(z + ring - 1, ring)}
    ways = (up, down)
    mate = {"c": 1 - c}
    sides = ({"px": 1 - px}, {"py": 1 - py})
    mine = (px, py)

    def far_slot(way, d):
        return lax.rem(z + ring - d, ring) if way == 0 else lax.rem(z + d, ring)

    def copy(src, dst, ssem, rsem, dev):
        return pltpu.make_async_remote_copy(
            src_ref=src, dst_ref=dst, send_sem=ssem, recv_sem=rsem, device_id=dev, device_id_type=MESH
        )

    barrier = pltpu.get_barrier_semaphore()
    for dev in (up, down, mate, *sides):
        pl.semaphore_signal(barrier, inc=1, device_id=dev, device_id_type=MESH)

    own_k = [
        pltpu.make_async_copy(
            rows_hbm.at[pl.ds(0, cache)], keys.at[pl.ds(rank * cache, cache)], local_sem.at[0]
        ),
        pltpu.make_async_copy(
            rows_hbm.at[pl.ds(cache, tok)],
            keys.at[pl.ds(cached_all + rank * tok, tok)],
            local_sem.at[1],
        ),
    ]
    own_w = [
        pltpu.make_async_copy(wk_hbm, w.at[rank, 0], local_sem.at[2]),
        pltpu.make_async_copy(wv_hbm, w.at[rank, 1], local_sem.at[3]),
    ]
    own_q = pltpu.make_async_copy(q_hbm, q, local_sem.at[4])
    for item in (*own_k, *own_w, own_q):
        item.start()
    pl.semaphore_wait(barrier, 5)

    def k_rows(zz, core, part):
        slot = zz * 2 + core
        if part == 0:
            return keys.at[pl.ds(slot * cache, cache)]
        return keys.at[pl.ds(cached_all + slot * tok, tok)]

    def k_ring(way, d, part):
        ref = k_rows(far_slot(way, d), c, part)
        return copy(ref, ref, kr_s.at[way, d, part], kr_r.at[way, d + 1, part], ways[way])

    def k_ring_in(way, d, part):
        ref = k_rows(far_slot(way, d), c, part)
        return copy(ref, ref, kr_s.at[way, d, part], kr_r.at[way, d, part], ways[way])

    def k_core(way, d, part):
        ref = k_rows(far_slot(way, d), c, part)
        return copy(ref, ref, kc_s.at[way, d, part], kc_r.at[way, d, part], mate)

    def k_core_in(way, d, part):
        ref = k_rows(far_slot(way, d), 1 - c, part)
        return copy(ref, ref, kc_s.at[way, d, part], kc_r.at[way, d, part], mate)

    def w_half(zz, core, m, half):
        return w.at[zz * 2 + core, m, pl.ds(half * half_rows, half_rows)]

    def w_ring(way, d, m):
        ref = w_half(far_slot(way, d), c, m, mine[m])
        return copy(ref, ref, wr_s.at[way, d, m], wr_r.at[way, d + 1, m], ways[way])

    def w_ring_in(way, d, m):
        ref = w_half(far_slot(way, d), c, m, mine[m])
        return copy(ref, ref, wr_s.at[way, d, m], wr_r.at[way, d, m], ways[way])

    def w_side(way, d, m):
        ref = w_half(far_slot(way, d), c, m, mine[m])
        return copy(ref, ref, wx_s.at[way, d, m], wx_r.at[way, d, m], sides[m])

    def w_side_in(way, d, m):
        ref = w_half(far_slot(way, d), c, m, 1 - mine[m])
        return copy(ref, ref, wx_s.at[way, d, m], wx_r.at[way, d, m], sides[m])

    def w_core(way, d, m):
        ref = w.at[far_slot(way, d) * 2 + c, m]
        return copy(ref, ref, wc_s.at[way, d, m], wc_r.at[way, d, m], mate)

    def w_core_in(way, d, m):
        ref = w.at[far_slot(way, d) * 2 + (1 - c), m]
        return copy(ref, ref, wc_s.at[way, d, m], wc_r.at[way, d, m], mate)

    for part in (0, 1):
        own_k[part].wait()
        k_ring(0, 0, part).start()
        k_ring(1, 0, part).start()
        k_core(0, 0, part).start()
    for m in (0, 1):
        own_w[m].wait()
        w_core(0, 0, m).start()

    def k_step(d, carry):
        for part in (0, 1):
            for way in (0, 1):
                k_ring_in(way, d, part).wait_recv()
                if carry is None:
                    k_ring(way, d, part).start()
                else:

                    @pl.when(jnp.logical_or(d < far - 1, part == way))
                    def _():
                        k_ring(way, d, part).start()

                k_core(way, d, part).start()
        return carry

    lax.fori_loop(1, far, k_step, 0)

    for m in (0, 1):
        for way in (0, 1):
            w_ring(way, 0, m).start()
    for part in (0, 1):
        k_ring_in(part, far, part).wait_recv()
        k_core(part, far, part).start()
    own_q.wait()

    lane = lax.broadcasted_iota(jnp.int32, (tok, ROPE), 1)
    ones_lane = jnp.where(lane == 0, 1.0, 0.0).astype(jnp.bfloat16)
    scale = math.log2(math.e) / math.sqrt(NOPE + ROPE)
    blocks = cached_all // BLOCK + (rank * tok) // BLOCK + 1
    rows_all = 2 * heads * tok

    def unit(zz, before_values):
        for core in (0, 1):
            slot = zz * 2 + core
            wide = heads * (NOPE + ROPE)
            block = q[:, pl.ds(pl.multiple_of(slot * wide, 128), wide)]
            for j in range(heads):
                at = j * (NOPE + ROPE)
                row = (core * heads + j) * tok
                lat = lax.dot_general(
                    block[:, at : at + NOPE],
                    w[slot, 0, :, j * NOPE : (j + 1) * NOPE],
                    NT,
                    preferred_element_type=jnp.float32,
                )
                qs[row : row + tok, :LATENT] = (lat * scale).astype(jnp.bfloat16)
                rot = block[:, at + NOPE : at + NOPE + ROPE].astype(jnp.float32)
                swapped = jnp.concatenate([rot[:, ROPE // 2 :], rot[:, : ROPE // 2]], 1)
                turned = (rot * turn_ref[:, :ROPE] + swapped * turn_ref[:, ROPE:]) * scale
                qs[row : row + tok, LATENT:] = jnp.concatenate(
                    [turned.astype(jnp.bfloat16), ones_lane], 1
                )

        def score(kb):
            first = pl.multiple_of(kb * BLOCK, BLOCK)
            return lax.dot_general(
                qs[...], keys[pl.ds(first, BLOCK), :], NT, preferred_element_type=jnp.float32
            )

        def lanes_max(s):
            best = s[:, :128]
            for n in range(1, BLOCK // 128):
                best = jnp.maximum(best, s[:, n * 128 : (n + 1) * 128])
            return best

        last = blocks - 1
        s = score(last)
        key_at = lax.broadcasted_iota(jnp.int32, (rows_all, BLOCK), 1)
        row_at = lax.rem(lax.broadcasted_iota(jnp.int32, (rows_all, BLOCK), 0), tok)
        edge = lax.rem(rank * tok, BLOCK)
        s = jnp.where(key_at <= row_at + edge, s, DEAD)
        scores[:, pl.ds(pl.multiple_of(last * BLOCK, BLOCK), BLOCK)] = s
        top[...] = lanes_max(s)

        def score_step(kb, carry):
            s = score(kb)
            scores[:, pl.ds(pl.multiple_of(kb * BLOCK, BLOCK), BLOCK)] = s
            top[...] = jnp.maximum(top[...], lanes_max(s))
            return carry

        lax.fori_loop(0, last, score_step, 0)
        best = jnp.max(top[...], axis=1, keepdims=True)
        top[...] = jnp.broadcast_to(best, top.shape)
        total[...] = jnp.zeros_like(total)
        acc[...] = jnp.zeros_like(acc)

        def value_step(kb, carry):
            first = pl.multiple_of(kb * BLOCK, BLOCK)
            parts = []
            best = top[...]
            run = total[...]
            for n in range(BLOCK // 128):
                p = jnp.exp2(scores[:, pl.ds(pl.multiple_of(first + n * 128, 128), 128)] - best)
                run = run + p
                parts.append(p.astype(jnp.bfloat16))
            total[...] = run
            weights = jnp.concatenate(parts, 1)
            acc[...] += jnp.dot(
                weights, keys[pl.ds(first, BLOCK), :LATENT], preferred_element_type=jnp.float32
            )
            return carry

        lax.fori_loop(0, blocks, value_step, 0)
        norm = 1.0 / jnp.sum(total[...], axis=1, keepdims=True)
        before_values()
        for core in (0, 1):
            slot = zz * 2 + core
            done = []
            for j in range(heads):
                row = (core * heads + j) * tok
                mixed = (acc[row : row + tok, :] * norm[row : row + tok]).astype(jnp.bfloat16)
                done.append(
                    jnp.dot(
                        mixed,
                        w[slot, 1, :, j * VH : (j + 1) * VH],
                        preferred_element_type=jnp.float32,
                    ).astype(jnp.bfloat16)
                )
            width = heads * VH
            out_ref[:, pl.ds(pl.multiple_of(slot * width, 128), width)] = jnp.concatenate(done, 1)

    def w_in(d, m, both=True):
        for way in (0, 1) if both else (m,):
            w_ring_in(way, d, m).wait_recv()
            if both:

                @pl.when(jnp.logical_or(d < far - 1, m == way))
                def _():
                    w_ring(way, d, m).start()

            w_side(way, d, m).start()

    def w_share(d, m, both=True):
        for way in (0, 1) if both else (m,):
            w_side_in(way, d, m).wait_recv()
            w_core(way, d, m).start()

    def waited_unit(way, e, value_way=None):
        w_core_in(way, e, 0).wait_recv()
        use = way if value_way is None else value_way
        unit(far_slot(way, e), lambda: w_core_in(use, e, 1).wait_recv())

    w_in(1, 0)
    for part in (0, 1):
        k_core_in(0, 0, part).wait_recv()

    def k_rest(d, carry):
        for part in (0, 1):
            for way in (0, 1):
                k_core_in(way, d, part).wait_recv()
        return carry

    lax.fori_loop(1, far, k_rest, 0)
    for part in (0, 1):
        k_core_in(part, far, part).wait_recv()
    w_in(1, 1)

    w_in(2, 0)
    w_share(1, 0)
    waited_unit(0, 0)
    w_in(2, 1)
    w_share(1, 1)

    def stage(d, carry):
        w_in(d, 0)
        w_share(d - 1, 0)
        waited_unit(0, d - 2)
        w_in(d, 1)
        w_share(d - 1, 1)
        waited_unit(1, d - 2)
        return carry

    lax.fori_loop(3, far, stage, 0)
    w_in(far, 0, False)
    w_share(far - 1, 0)
    waited_unit(0, far - 2)
    w_in(far, 1, False)
    w_share(far - 1, 1)
    w_share(far, 0, False)
    waited_unit(1, far - 2)
    w_share(far, 1, False)
    waited_unit(0, far - 1)
    waited_unit(1, far - 1)
    waited_unit(0, far, 1)

    for part in (0, 1):
        k_core(0, 0, part).wait_send()
        w_core(0, 0, part).wait_send()
        for way in (0, 1):
            k_ring(way, 0, part).wait_send()
            w_ring(way, 0, part).wait_send()

    def drain(d, carry):
        for part in (0, 1):
            for way in (0, 1):

                @pl.when(jnp.logical_or(d < far - 1, part == way))
                def _():
                    k_ring(way, d, part).wait_send()
                    w_ring(way, d, part).wait_send()

                k_core(way, d, part).wait_send()
                w_core(way, d, part).wait_send()
                w_side(way, d, part).wait_send()
        return carry

    lax.fori_loop(1, far, drain, 0)
    for part in (0, 1):
        k_core(part, far, part).wait_send()
        w_core(part, far, part).wait_send()
        w_side(part, far, part).wait_send()


def phases_for(positions, rope_width):
    half_width = rope_width // 2
    inverse = 10000.0 ** (-(jnp.arange(half_width, dtype=jnp.float32) * 2.0) / rope_width)
    return positions.astype(jnp.float32)[:, None] * inverse[None, :]


def local(queries, kv_new, kv_cache, kv_gain, w_key, w_value, prefix_len):
    ring = lax.axis_size("z")
    rank = lax.axis_index(SEQ)
    tok = queries.shape[0]
    cache = kv_cache.shape[0]
    heads = w_key.shape[1] // NOPE
    start = prefix_len[0]
    positions = start + rank * tok + jnp.arange(tok, dtype=jnp.int32)
    phases = phases_for(positions, ROPE)
    cosine, sine = jnp.cos(phases), jnp.sin(phases)
    turn = jnp.concatenate([cosine, cosine, -sine, sine], 1)
    raw = kv_new[:, :LATENT].astype(jnp.float32)
    inv_rms = lax.rsqrt(jnp.mean(raw * raw, axis=1, keepdims=True) + EPSILON)
    latent = (raw * inv_rms * kv_gain[None, :]).astype(jnp.bfloat16)
    rot = kv_new[:, LATENT:].astype(jnp.float32)
    swapped = jnp.concatenate([rot[:, ROPE // 2 :], rot[:, : ROPE // 2]], 1)
    rope = (rot * turn[:, :ROPE] + swapped * turn[:, ROPE:]).astype(jnp.bfloat16)
    pad = WIDE - LATENT - ROPE
    new_rows = jnp.concatenate([latent, rope, jnp.zeros((tok, pad), jnp.bfloat16)], 1)
    index = rank * cache + jnp.arange(cache, dtype=jnp.int32)[:, None]
    spare = jnp.arange(pad, dtype=jnp.int32)[None, :]
    bias = jnp.where((index >= start) & (spare == 0), DEAD, 0.0).astype(jnp.bfloat16)
    rows = jnp.concatenate([jnp.concatenate([kv_cache, bias], 1), new_rows], 0)
    slots = 2 * ring
    keys_all = slots * (cache + tok)
    rows_all = 2 * heads * tok
    hbm = pl.BlockSpec(memory_space=pl.ANY)
    vmem = pl.BlockSpec(memory_space=pltpu.VMEM)
    sems = pltpu.SemaphoreType.DMA((2, ring // 2 + 1, 2))
    out = pl.pallas_call(
        functools.partial(kernel, (ring, tok, cache, heads)),
        out_shape=jax.ShapeDtypeStruct((tok, slots * heads * VH), jnp.bfloat16),
        in_specs=[hbm, hbm, hbm, hbm, vmem],
        out_specs=vmem,
        scratch_shapes=[
            pltpu.VMEM((slots, 2, LATENT, heads * NOPE), jnp.bfloat16),
            pltpu.VMEM((keys_all, WIDE), jnp.bfloat16),
            pltpu.VMEM(queries.shape, jnp.bfloat16),
            pltpu.VMEM((rows_all, WIDE), jnp.bfloat16),
            pltpu.VMEM((rows_all, keys_all), jnp.float32),
            pltpu.VMEM((rows_all, LATENT), jnp.float32),
            pltpu.VMEM((rows_all, 128), jnp.float32),
            pltpu.VMEM((rows_all, 128), jnp.float32),
            pltpu.SemaphoreType.DMA((5,)),
        ]
        + [sems] * 10,
        compiler_params=pltpu.CompilerParams(
            collective_id=0, has_side_effects=True, vmem_limit_bytes=66 * 1000 * 1000
        ),
        name="attend",
    )(queries, rows, w_key, w_value, turn)
    return out


def solution(mesh):
    side = math.isqrt(mesh.shape["groups"])
    ring = mesh.shape["seq"] // 2
    torus = Mesh(mesh.devices.reshape(side // 2, 2, side // 2, 2, ring, 2), AXES)
    tokens = P((*GROUPS, *SEQ), None)
    placed = (tokens, tokens, tokens, P(), P(None, SEQ), P(None, SEQ), P(GROUPS))
    return jax.shard_map(local, mesh=torus, in_specs=placed, out_specs=tokens, check_vma=False)
```

time: 582 us -> 197 us (0.34)
  the two profiles are of different devices: /device:TPU:86 before, /device:TPU:1732 now
where the time goes in v1:
time: 197 us; the launch traced here: 196 us
  Pallas kernels  187 us (95%)
  other arithmetic  5.94 us (3%)
  local copies, waits for them, and re-layouts  3.05 us (2%)
    pallas_call x1, Pallas kernels, local(): pl.pallas_call(functools.partial(kernel, (ring, tok, cache, heads)), out_...  187 us

profile of v1, /device:TPU:1732, one launch (start us, length us, event | category | flops | bytes accessed | tf_op | source)
XLA Modules:
  0.0 196.4 jit_solution(5733832030690167404)
XLA Ops:
  0.7 1.0 fusion
  1.7 0.1 select_convert_fusion
  1.8 0.7 slice_convert_fusion
  2.5 0.9 fusion.2
  3.4 0.2 fusion.5
  3.6 0.8 fusion.4
  4.4 0.7 pad_maximum_fusion.turn_ref
  5.1 1.5 maximum_maximum_fusion.rows_hbm
  6.7 186.7 %attend.1 = bf16[64,16384]{1,0:T(8,128)(2,1)} custom-call(bf16[64,24576]{1,0:T(8,128)(2,1)} %q_hbm.1, bf16[96,640]{1,0:T(8,128)(2,1)} %maximum_maximum_fusion.rows_hbm, bf16[512,512]{1,0:T(8,128)(2,1)} %wk_hbm.1, bf16[512,512]{1,0:T(8,128)(2,1)} %wv_hbm.1, f32[64,128]{1,0:T(8,128)} %pad_maximum_fusion.turn_ref), custom_call_target="tpu_custom_call" | custom-call | tf_op jit(solution)/shard_map/attend/pallas_call | solution.py:408
  193.4 3.0 %copy.10 = bf16[64,16384]{1,0:T(8,128)(2,1)} copy(bf16[64,16384]{1,0:T(8,128)(2,1)} %attend.1) | data formatting | bytes 4194304
  (6 shorter events, 0.0 us)

commit v2 on v1

v2 whole, which is shorter than its diff:
```python
import functools
import math

import jax
import jax.numpy as jnp
from jax import lax
from jax.experimental import pallas as pl
from jax.experimental.pallas import tpu as pltpu
from jax.sharding import Mesh
from jax.sharding import PartitionSpec as P

NOPE = 128
ROPE = 64
LATENT = 512
VH = 128
WIDE = 640
BLOCK = 1024
LANES = 128
AXES = ("gx", "px", "gy", "py", "z", "c")
GROUPS = ("gx", "px", "gy", "py")
SEQ = ("z", "c")
EPSILON = 1e-06
DEAD = -1e30
MESH = pl.DeviceIdType.MESH
NT = (((1,), (1,)), ((), ()))


def kernel(
    dims,
    q_hbm,
    rows_hbm,
    wk_hbm,
    wv_hbm,
    turn_ref,
    out_hbm,
    w,
    keys,
    q,
    qs,
    scores,
    made,
    local_sem,
    ql_sem,
    ol_sem,
    q_s,
    q_r,
    o_s,
    o_r,
    kr_s,
    kr_r,
    kc_s,
    kc_r,
    wr_s,
    wr_r,
    wx_s,
    wx_r,
):
    ring, tok, cache, heads = dims
    far = ring // 2
    units = ring
    z = lax.axis_index("z")
    c = lax.axis_index("c")
    px = lax.axis_index("px")
    py = lax.axis_index("py")
    rank = z * 2 + c
    cached_all = ring * 2 * cache
    keys_all = cached_all + ring * 2 * tok
    chip = 2 * tok
    half_rows = LATENT // 2
    q_wide = heads * (NOPE + ROPE)
    o_wide = heads * VH
    up = {"z": lax.rem(z + 1, ring)}
    down = {"z": lax.rem(z + ring - 1, ring)}
    ways = (up, down)
    mate = {"c": 1 - c}
    sides = ({"px": 1 - px}, {"py": 1 - py})
    mine = (px, py)

    def far_slot(way, d):
        return lax.rem(z + ring + (2 * way - 1) * d, ring)

    def copy(src, dst, ssem, rsem, dev):
        return pltpu.make_async_remote_copy(
            src_ref=src, dst_ref=dst, send_sem=ssem, recv_sem=rsem, device_id=dev, device_id_type=MESH
        )

    barrier = pltpu.get_barrier_semaphore()
    for dev in (up, down, mate, *sides):
        pl.semaphore_signal(barrier, inc=1, device_id=dev, device_id_type=MESH)

    own_k = [
        pltpu.make_async_copy(
            rows_hbm.at[pl.ds(0, cache)], keys.at[pl.ds(rank * cache, cache)], local_sem.at[0]
        ),
        pltpu.make_async_copy(
            rows_hbm.at[pl.ds(cache, tok)],
            keys.at[pl.ds(cached_all + rank * tok, tok)],
            local_sem.at[1],
        ),
    ]
    own_w = [
        pltpu.make_async_copy(wk_hbm, w.at[z, 0], local_sem.at[2]),
        pltpu.make_async_copy(wv_hbm, w.at[z, 1], local_sem.at[3]),
    ]
    for item in (*own_k, *own_w):
        item.start()

    def q_from(zz, core):
        return q_hbm.at[:, pl.ds(pl.multiple_of((zz * 2 + core) * q_wide, LANES), q_wide)]

    def q_into(zz, core):
        return q.at[pl.ds(core * tok, tok), pl.ds(pl.multiple_of(zz * q_wide, LANES), q_wide)]

    def q_own(zz):
        return pltpu.make_async_copy(q_from(zz, c), q_into(zz, c), ql_sem.at[zz])

    def q_out(zz):
        return copy(q_from(zz, 1 - c), q_into(zz, c), q_s.at[zz], q_r.at[zz], mate)

    def q_in(zz):
        return copy(q_from(zz, c), q_into(zz, 1 - c), q_s.at[zz], q_r.at[zz], mate)

    def k_rows(zz, core, part):
        slot = zz * 2 + core
        if part == 0:
            return keys.at[pl.ds(slot * cache, cache)]
        return keys.at[pl.ds(cached_all + slot * tok, tok)]

    def k_ring(way, d, part):
        ref = k_rows(far_slot(way, d), c, part)
        return copy(ref, ref, kr_s.at[way, d, part], kr_r.at[way, d + 1, part], ways[way])

    def k_ring_in(way, d, part):
        ref = k_rows(far_slot(way, d), c, part)
        return copy(ref, ref, kr_s.at[way, d, part], kr_r.at[way, d, part], ways[way])

    def k_core(way, d, part):
        ref = k_rows(far_slot(way, d), c, part)
        return copy(ref, ref, kc_s.at[way, d, part], kc_r.at[way, d, part], mate)

    def k_core_in(way, d, part):
        ref = k_rows(far_slot(way, d), 1 - c, part)
        return copy(ref, ref, kc_s.at[way, d, part], kc_r.at[way, d, part], mate)

    def w_half(zz, m, half):
        return w.at[zz, m, pl.ds(half * half_rows, half_rows)]

    def w_ring(way, d, m):
        ref = w_half(far_slot(way, d), m, mine[m])
        return copy(ref, ref, wr_s.at[way, d, m], wr_r.at[way, d + 1, m], ways[way])

    def w_ring_in(way, d, m):
        ref = w_half(far_slot(way, d), m, mine[m])
        return copy(ref, ref, wr_s.at[way, d, m], wr_r.at[way, d, m], ways[way])

    def w_side(way, d, m):
        ref = w_half(far_slot(way, d), m, mine[m])
        return copy(ref, ref, wx_s.at[way, d, m], wx_r.at[way, d, m], sides[m])

    def w_side_in(way, d, m):
        ref = w_half(far_slot(way, d), m, 1 - mine[m])
        return copy(ref, ref, wx_s.at[way, d, m], wx_r.at[way, d, m], sides[m])

    slice_rows = half_rows // far

    def w_slice(way, n):
        ref = w.at[z, 0, pl.ds(mine[0] * half_rows + n * slice_rows, slice_rows)]
        return copy(ref, ref, wr_s.at[way, 0, 0], wr_r.at[way, 1, 0], ways[way])

    pl.semaphore_wait(barrier, 5)
    for part in (0, 1):
        own_k[part].wait()
        k_ring(0, 0, part).start()
        k_ring(1, 0, part).start()
        k_core(0, 0, part).start()
    own_w[0].wait()
    for way in (0, 1):
        w_slice(way, 0).start()

    def q_start(zz, carry):
        q_own(zz).start()
        q_out(zz).start()
        return carry

    lax.fori_loop(0, units, q_start, 0)

    def k_step(d, carry):
        for part in (0, 1):
            for way in (0, 1):
                k_ring_in(way, d, part).wait_recv()

                @pl.when(jnp.logical_or(d < far - 1, part == way))
                def _():
                    k_ring(way, d, part).start()

                k_core(way, d, part).start()
        for way in (0, 1):
            w_slice(way, d).start()
        return carry

    lax.fori_loop(1, far, k_step, 0)
    own_w[1].wait()
    for way in (0, 1):
        w_ring(way, 0, 1).start()
    for part in (0, 1):
        k_ring_in(part, far, part).wait_recv()
        k_core(part, far, part).start()

    def q_end(zz, carry):
        q_own(zz).wait()
        q_in(zz).wait_recv()
        return carry

    lax.fori_loop(0, units, q_end, 0)

    lane = lax.broadcasted_iota(jnp.int32, (chip, ROPE), 1)
    ones_lane = jnp.where(lane == 0, 1.0, 0.0).astype(jnp.bfloat16)
    scale = math.log2(math.e) / math.sqrt(NOPE + ROPE)

    def unit(zz, turn, before_values):
        block = q[:, pl.ds(pl.multiple_of(zz * q_wide, LANES), q_wide)]
        for j in range(heads):
            at = j * (NOPE + ROPE)
            row = j * chip
            lat = lax.dot_general(
                block[:, at : at + NOPE],
                w[zz, 0, :, j * NOPE : (j + 1) * NOPE],
                NT,
                preferred_element_type=jnp.float32,
            )
            qs[row : row + chip, :LATENT] = (lat * scale).astype(jnp.bfloat16)
            rot = block[:, at + NOPE : at + NOPE + ROPE].astype(jnp.float32)
            swapped = jnp.concatenate([rot[:, ROPE // 2 :], rot[:, : ROPE // 2]], 1)
            turned = (rot * turn_ref[:, :ROPE] + swapped * turn_ref[:, ROPE:]) * scale
            qs[row : row + chip, LATENT:] = jnp.concatenate(
                [turned.astype(jnp.bfloat16), ones_lane], 1
            )

        down_by = lax.broadcasted_iota(jnp.int32, (chip, LANES), 0) - lax.broadcasted_iota(
            jnp.int32, (chip, LANES), 1
        )
        down_by = jnp.concatenate([down_by] * heads, 0)
        best = None
        for first in range(0, keys_all, BLOCK):
            s = lax.dot_general(
                qs[...], keys[first : first + BLOCK, :], NT, preferred_element_type=jnp.float32
            )
            for n in range(0, BLOCK, LANES):
                tile = s[:, n : n + LANES]
                owner = (first + n - cached_all) // chip
                if owner >= 0:
                    tile = jnp.where(down_by >= (owner - z) * chip, tile, DEAD)
                scores[:, first + n : first + n + LANES] = tile
                best = tile if best is None else jnp.maximum(best, tile)
        best = jnp.broadcast_to(jnp.max(best, axis=1, keepdims=True), best.shape)
        total = None
        parts = []
        for first in range(0, keys_all, LANES):
            p = jnp.exp2(scores[:, first : first + LANES] - best)
            total = p if total is None else total + p
            parts.append(p.astype(jnp.bfloat16))
        acc = jnp.dot(
            jnp.concatenate(parts, 1), keys[:, :LATENT], preferred_element_type=jnp.float32
        )
        norm = 1.0 / jnp.sum(total, axis=1, keepdims=True)
        mixed = (acc * norm).astype(jnp.bfloat16)
        before_values()
        for j in range(heads):
            made[turn, :, j * VH : (j + 1) * VH] = jnp.dot(
                mixed[j * chip : (j + 1) * chip],
                w[zz, 1, :, j * VH : (j + 1) * VH],
                preferred_element_type=jnp.float32,
            ).astype(jnp.bfloat16)

    def w_in(d, m):
        for way in (0, 1):

            @pl.when(jnp.logical_or(d < far, m == way))
            def _():
                w_ring_in(way, d, m).wait_recv()

                @pl.when(jnp.logical_or(d < far - 1, jnp.logical_and(d < far, m == way)))
                def _():
                    w_ring(way, d, m).start()

                w_side(way, d, m).start()

    def chip_of(u):
        return far_slot(1 - lax.rem(u, 2), (u + 1) // 2)

    def o_into(u, core):
        slot = chip_of(u) * 2 + core
        return out_hbm.at[:, pl.ds(pl.multiple_of(slot * o_wide, LANES), o_wide)]

    def o_own(u):
        return pltpu.make_async_copy(
            made.at[u, pl.ds(c * tok, tok)], o_into(u, c), ol_sem.at[u]
        )

    def o_out(u):
        return copy(made.at[u, pl.ds((1 - c) * tok, tok)], o_into(u, c), o_s.at[u], o_r.at[u], mate)

    def o_in(u):
        return copy(made.at[u, pl.ds(c * tok, tok)], o_into(u, 1 - c), o_s.at[u], o_r.at[u], mate)

    for part in (0, 1):
        k_core_in(0, 0, part).wait_recv()

    def k_rest(d, carry):
        for part in (0, 1):
            for way in (0, 1):
                k_core_in(way, d, part).wait_recv()
        return carry

    lax.fori_loop(1, far, k_rest, 0)
    for part in (0, 1):
        k_core_in(part, far, part).wait_recv()
    w_in(1, 0)

    def step(u, carry):
        e = (u + 1) // 2
        odd = lax.rem(u, 2) == 1

        @pl.when(u == 1)
        def _():
            w_in(1, 1)

        for m in (0, 1):

            @pl.when(jnp.logical_and(odd == (m == 0), jnp.logical_and(u > 0, u < units - 1)))
            def _():
                w_in(e + 1, m)

        @pl.when(u > 0)
        def _():
            o_own(u - 1).start()
            o_out(u - 1).start()
            w_side_in(1 - lax.rem(u, 2), e, 0).wait_recv()

        def before_values():
            way = 1 - lax.rem(u, 2) + (u + 1) // units

            @pl.when(u > 0)
            def _():
                w_side_in(way, e, 1).wait_recv()

        unit(chip_of(u), u, before_values)
        return carry

    lax.fori_loop(0, units, step, 0)
    o_own(units - 1).start()
    o_out(units - 1).start()

    for part in (0, 1):
        k_core(0, 0, part).wait_send()
        for way in (0, 1):
            k_ring(way, 0, part).wait_send()
            w_ring(way, 0, part).wait_send()

    def drain(d, carry):
        for part in (0, 1):
            for way in (0, 1):

                @pl.when(jnp.logical_or(d < far - 1, part == way))
                def _():
                    k_ring(way, d, part).wait_send()
                    w_ring(way, d, part).wait_send()

                k_core(way, d, part).wait_send()
                w_side(way, d, part).wait_send()
        return carry

    lax.fori_loop(1, far, drain, 0)
    for part in (0, 1):
        k_core(part, far, part).wait_send()
        w_side(part, far, part).wait_send()

    def finish(u, carry):
        q_out(u).wait_send()
        o_own(u).wait()
        o_out(u).wait_send()
        o_in(u).wait_recv()
        return carry

    lax.fori_loop(0, units, finish, 0)


def phases_for(positions, rope_width):
    half_width = rope_width // 2
    inverse = 10000.0 ** (-(jnp.arange(half_width, dtype=jnp.float32) * 2.0) / rope_width)
    return positions.astype(jnp.float32)[:, None] * inverse[None, :]


def local(queries, kv_new, kv_cache, kv_gain, w_key, w_value, prefix_len):
    ring = lax.axis_size("z")
    rank = lax.axis_index(SEQ)
    tok = queries.shape[0]
    cache = kv_cache.shape[0]
    heads = w_key.shape[1] // NOPE
    start = prefix_len[0]
    base = start + lax.axis_index("z") * (2 * tok)
    phases = phases_for(base + jnp.arange(2 * tok, dtype=jnp.int32), ROPE)
    cosine, sine = jnp.cos(phases), jnp.sin(phases)
    turns = jnp.concatenate([cosine, cosine, -sine, sine], 1)
    turn = lax.dynamic_slice_in_dim(turns, lax.axis_index("c") * tok, tok, 0)
    raw = kv_new[:, :LATENT].astype(jnp.float32)
    inv_rms = lax.rsqrt(jnp.mean(raw * raw, axis=1, keepdims=True) + EPSILON)
    latent = (raw * inv_rms * kv_gain[None, :]).astype(jnp.bfloat16)
    rot = kv_new[:, LATENT:].astype(jnp.float32)
    swapped = jnp.concatenate([rot[:, ROPE // 2 :], rot[:, : ROPE // 2]], 1)
    rope = (rot * turn[:, :ROPE] + swapped * turn[:, ROPE:]).astype(jnp.bfloat16)
    pad = WIDE - LATENT - ROPE
    new_rows = jnp.concatenate([latent, rope, jnp.zeros((tok, pad), jnp.bfloat16)], 1)
    index = rank * cache + jnp.arange(cache, dtype=jnp.int32)[:, None]
    spare = jnp.arange(pad, dtype=jnp.int32)[None, :]
    bias = jnp.where((index >= start) & (spare == 0), DEAD, 0.0).astype(jnp.bfloat16)
    rows = jnp.concatenate([jnp.concatenate([kv_cache, bias], 1), new_rows], 0)
    slots = 2 * ring
    keys_all = slots * (cache + tok)
    rows_all = 2 * heads * tok
    hbm = pl.BlockSpec(memory_space=pl.ANY)
    vmem = pl.BlockSpec(memory_space=pltpu.VMEM)
    each = pltpu.SemaphoreType.DMA((ring,))
    sems = pltpu.SemaphoreType.DMA((2, ring // 2 + 1, 2))
    return pl.pallas_call(
        functools.partial(kernel, (ring, tok, cache, heads)),
        out_shape=jax.ShapeDtypeStruct((tok, slots * heads * VH), jnp.bfloat16),
        in_specs=[hbm, hbm, hbm, hbm, vmem],
        out_specs=hbm,
        scratch_shapes=[
            pltpu.VMEM((ring, 2, LATENT, heads * NOPE), jnp.bfloat16),
            pltpu.VMEM((keys_all, WIDE), jnp.bfloat16),
            pltpu.VMEM((2 * tok, ring * heads * (NOPE + ROPE)), jnp.bfloat16),
            pltpu.VMEM((rows_all, WIDE), jnp.bfloat16),
            pltpu.VMEM((rows_all, keys_all), jnp.float32),
            pltpu.VMEM((ring, 2 * tok, heads * VH), jnp.bfloat16),
            pltpu.SemaphoreType.DMA((4,)),
        ]
        + [each] * 6
        + [sems] * 8,
        compiler_params=pltpu.CompilerParams(
            collective_id=0, has_side_effects=True, vmem_limit_bytes=66 * 1000 * 1000
        ),
        name="attend",
    )(queries, rows, w_key, w_value, turns)


def solution(mesh):
    side = math.isqrt(mesh.shape["groups"])
    ring = mesh.shape["seq"] // 2
    torus = Mesh(mesh.devices.reshape(side // 2, 2, side // 2, 2, ring, 2), AXES)
    tokens = P((*GROUPS, *SEQ), None)
    placed = (tokens, tokens, tokens, P(), P(None, SEQ), P(None, SEQ), P(GROUPS))
    return jax.shard_map(local, mesh=torus, in_specs=placed, out_specs=tokens, check_vma=False)
```

time: 197 us -> 158 us (0.80)
  the two profiles are of different devices: /device:TPU:1732 before, /device:TPU:86 now
where the time goes in v2:
time: 158 us; the launch traced here: 156 us
  Pallas kernels  146 us (92%)
  other arithmetic  5.51 us (3%)
  local copies, waits for them, and re-layouts  3.13 us (2%)
    pallas_call x1, Pallas kernels, local(): pl.pallas_call(functools.partial(kernel, (ring, tok, cache, heads)), out_...  146 us

profile of v2, /device:TPU:86, one launch (start us, length us, event | category | flops | bytes accessed | tf_op | source)
XLA Modules:
  0.0 155.7 jit_solution(12086662496454805963)
XLA Ops:
  0.7 1.0 fusion
  1.7 0.1 select_convert_fusion
  1.8 0.7 slice_convert_fusion
  2.5 0.1 fusion.6
  2.6 0.9 fusion.2
  3.5 0.3 multiply_cosine_fusion
  3.8 0.1 pad_maximum_fusion.turn_ref
  3.9 0.0 copy-start
  4.0 0.8 fusion.4
  4.8 1.5 maximum_maximum_fusion.rows_hbm
  6.3 0.0 copy-done
  6.3 146.4 %attend.1 = bf16[64,16384]{1,0:T(8,128)(2,1)} custom-call(bf16[64,24576]{1,0:T(8,128)(2,1)} %q_hbm.1, bf16[96,640]{1,0:T(8,128)(2,1)} %maximum_maximum_fusion.rows_hbm, bf16[512,512]{1,0:T(8,128)(2,1)} %wk_hbm.1, bf16[512,512]{1,0:T(8,128)(2,1)} %wv_hbm.1, f32[128,128]{1,0:T(8,128)} %copy-done), custom_call_target="tpu_custom_call" | custom-call | tf_op jit(solution)/shard_map/attend/pallas_call | solution.py:425
  152.7 3.0 %copy.11 = bf16[64,16384]{1,0:T(8,128)(2,1)} copy(bf16[64,16384]{1,0:T(8,128)(2,1)} %attend.1) | data formatting | bytes 4194304
  (6 shorter events, 0.0 us)
Async XLA Ops:
  3.9 2.4 %copy-start = (f32[128,128]{1,0:T(8,128)}, f32[128,128]{1,0:T(8,128)S(1)}, u32[]{:S(2)}) copy-start(f32[128,128]{1,0:T(8,128)S(1)} %pad_maximum_fusion.turn_ref) | copy-start | bytes 196612

commit v3 on v2

--- a/solution.py
+++ b/solution.py
@@ -27,15 +27,18 @@
 
 def kernel(
     dims,
+    start_ref,
     q_hbm,
-    rows_hbm,
+    new_ref,
+    cache_ref,
+    gain_ref,
     wk_hbm,
     wv_hbm,
-    turn_ref,
     out_hbm,
     w,
     keys,
     q,
+    turn_ref,
     qs,
     scores,
     made,
@@ -88,21 +91,11 @@
     for dev in (up, down, mate, *sides):
         pl.semaphore_signal(barrier, inc=1, device_id=dev, device_id_type=MESH)
 
-    own_k = [
-        pltpu.make_async_copy(
-            rows_hbm.at[pl.ds(0, cache)], keys.at[pl.ds(rank * cache, cache)], local_sem.at[0]
-        ),
-        pltpu.make_async_copy(
-            rows_hbm.at[pl.ds(cache, tok)],
-            keys.at[pl.ds(cached_all + rank * tok, tok)],
-            local_sem.at[1],
-        ),
+    own_w = [
+        pltpu.make_async_copy(wk_hbm, w.at[z, 0], local_sem.at[0]),
+        pltpu.make_async_copy(wv_hbm, w.at[z, 1], local_sem.at[1]),
     ]
-    own_w = [
-        pltpu.make_async_copy(wk_hbm, w.at[z, 0], local_sem.at[2]),
-        pltpu.make_async_copy(wv_hbm, w.at[z, 1], local_sem.at[3]),
-    ]
-    for item in (*own_k, *own_w):
+    for item in own_w:
         item.start()
 
     def q_from(zz, core):
@@ -161,21 +154,48 @@
         ref = w_half(far_slot(way, d), m, 1 - mine[m])
         return copy(ref, ref, wx_s.at[way, d, m], wx_r.at[way, d, m], sides[m])
 
-    slice_rows = half_rows // far
-
-    def w_slice(way, n):
-        ref = w.at[z, 0, pl.ds(mine[0] * half_rows + n * slice_rows, slice_rows)]
-        return copy(ref, ref, wr_s.at[way, 0, 0], wr_r.at[way, 1, 0], ways[way])
+    slice_rows = 2 * half_rows // far
+
+    def w_slice(way, m, n):
+        ref = w.at[z, m, pl.ds(mine[m] * half_rows + n * slice_rows, slice_rows)]
+        return copy(ref, ref, wr_s.at[way, 0, m], wr_r.at[way, 1, m], ways[way])
+
+    begin = start_ref[0]
+    half = ROPE // 2
+    wave = lax.broadcasted_iota(jnp.int32, (chip, LANES), 1)
+    inverse = jnp.exp(lax.rem(wave, half).astype(jnp.float32) * (-2.0 * math.log(10000.0) / ROPE))
+    place = begin + z * chip + lax.broadcasted_iota(jnp.int32, (chip, LANES), 0)
+    phases = place.astype(jnp.float32) * inverse
+    sine = jnp.sin(phases)
+    turn_ref[...] = jnp.where(
+        wave < ROPE, jnp.cos(phases), jnp.where(wave < ROPE + half, -sine, sine)
+    )
+    raw = new_ref[:, :LATENT].astype(jnp.float32)
+    inv_rms = lax.rsqrt(jnp.mean(raw * raw, axis=1, keepdims=True) + EPSILON)
+    new_at = pl.ds(pl.multiple_of(cached_all + rank * tok, tok), tok)
+    keys[new_at, :LATENT] = (raw * inv_rms * gain_ref[...]).astype(jnp.bfloat16)
+    rot = new_ref[:, LATENT:].astype(jnp.float32)
+    swapped = jnp.concatenate([rot[:, half:], rot[:, :half]], 1)
+    turn_own = turn_ref[pl.ds(pl.multiple_of(c * tok, tok), tok), :]
+    rope_new = (rot * turn_own[:, :ROPE] + swapped * turn_own[:, ROPE:]).astype(jnp.bfloat16)
+    pad = WIDE - LATENT - ROPE
+    keys[new_at, LATENT:] = jnp.concatenate([rope_new, jnp.zeros((tok, pad), jnp.bfloat16)], 1)
+    cache_at = pl.ds(pl.multiple_of(rank * cache, cache), cache)
+    keys[cache_at, :LATENT] = cache_ref[:, :LATENT]
+    spare = lax.broadcasted_iota(jnp.int32, (cache, pad), 1)
+    index = rank * cache + lax.broadcasted_iota(jnp.int32, (cache, pad), 0)
+    bias = jnp.where(jnp.logical_and(index >= begin, spare == 0), DEAD, 0.0).astype(jnp.bfloat16)
+    keys[cache_at, LATENT:] = jnp.concatenate([cache_ref[:, LATENT:], bias], 1)
 
     pl.semaphore_wait(barrier, 5)
     for part in (0, 1):
-        own_k[part].wait()
         k_ring(0, 0, part).start()
         k_ring(1, 0, part).start()
         k_core(0, 0, part).start()
-    own_w[0].wait()
+    for m in (0, 1):
+        own_w[m].wait()
     for way in (0, 1):
-        w_slice(way, 0).start()
+        w_slice(way, 0, 0).start()
 
     def q_start(zz, carry):
         q_own(zz).start()
@@ -194,14 +214,24 @@
                     k_ring(way, d, part).start()
 
                 k_core(way, d, part).start()
-        for way in (0, 1):
-            w_slice(way, d).start()
+        for m in (0, 1):
+
+            @pl.when(d // (far // 2) == m)
+            def _():
+                for way in (0, 1):
+                    w_slice(way, m, d - m * (far // 2)).start()
+
+        @pl.when(d == far - 2)
+        def _():
+            for way in (0, 1):
+                w_ring_in(way, 1, 0).wait_recv()
+                w_side(way, 1, 0).start()
+
         return carry
 
     lax.fori_loop(1, far, k_step, 0)
-    own_w[1].wait()
     for way in (0, 1):
-        w_ring(way, 0, 1).start()
+        w_ring(way, 1, 0).start()
     for part in (0, 1):
         k_ring_in(part, far, part).wait_recv()
         k_core(part, far, part).start()
@@ -315,7 +345,6 @@
     lax.fori_loop(1, far, k_rest, 0)
     for part in (0, 1):
         k_core_in(part, far, part).wait_recv()
-    w_in(1, 0)
 
     def step(u, carry):
         e = (u + 1) // 2
@@ -385,36 +414,11 @@
     lax.fori_loop(0, units, finish, 0)
 
 
-def phases_for(positions, rope_width):
-    half_width = rope_width // 2
-    inverse = 10000.0 ** (-(jnp.arange(half_width, dtype=jnp.float32) * 2.0) / rope_width)
-    return positions.astype(jnp.float32)[:, None] * inverse[None, :]
-
-
 def local(queries, kv_new, kv_cache, kv_gain, w_key, w_value, prefix_len):
     ring = lax.axis_size("z")
-    rank = lax.axis_index(SEQ)
     tok = queries.shape[0]
     cache = kv_cache.shape[0]
     heads = w_key.shape[1] // NOPE
-    start = prefix_len[0]
-    base = start + lax.axis_index("z") * (2 * tok)
-    phases = phases_for(base + jnp.arange(2 * tok, dtype=jnp.int32), ROPE)
-    cosine, sine = jnp.cos(phases), jnp.sin(phases)
-    turns = jnp.concatenate([cosine, cosine, -sine, sine], 1)
-    turn = lax.dynamic_slice_in_dim(turns, lax.axis_index("c") * tok, tok, 0)
-    raw = kv_new[:, :LATENT].astype(jnp.float32)
-    inv_rms = lax.rsqrt(jnp.mean(raw * raw, axis=1, keepdims=True) + EPSILON)
-    latent = (raw * inv_rms * kv_gain[None, :]).astype(jnp.bfloat16)
-    rot = kv_new[:, LATENT:].astype(jnp.float32)
-    swapped = jnp.concatenate([rot[:, ROPE // 2 :], rot[:, : ROPE // 2]], 1)
-    rope = (rot * turn[:, :ROPE] + swapped * turn[:, ROPE:]).astype(jnp.bfloat16)
-    pad = WIDE - LATENT - ROPE
-    new_rows = jnp.concatenate([latent, rope, jnp.zeros((tok, pad), jnp.bfloat16)], 1)
-    index = rank * cache + jnp.arange(cache, dtype=jnp.int32)[:, None]
-    spare = jnp.arange(pad, dtype=jnp.int32)[None, :]
-    bias = jnp.where((index >= start) & (spare == 0), DEAD, 0.0).astype(jnp.bfloat16)
-    rows = jnp.concatenate([jnp.concatenate([kv_cache, bias], 1), new_rows], 0)
     slots = 2 * ring
     keys_all = slots * (cache + tok)
     rows_all = 2 * heads * tok
@@ -425,16 +429,25 @@
     return pl.pallas_call(
         functools.partial(kernel, (ring, tok, cache, heads)),
         out_shape=jax.ShapeDtypeStruct((tok, slots * heads * VH), jnp.bfloat16),
-        in_specs=[hbm, hbm, hbm, hbm, vmem],
+        in_specs=[
+            pl.BlockSpec(memory_space=pltpu.SMEM),
+            hbm,
+            vmem,
+            vmem,
+            vmem,
+            hbm,
+            hbm,
+        ],
         out_specs=hbm,
         scratch_shapes=[
             pltpu.VMEM((ring, 2, LATENT, heads * NOPE), jnp.bfloat16),
             pltpu.VMEM((keys_all, WIDE), jnp.bfloat16),
             pltpu.VMEM((2 * tok, ring * heads * (NOPE + ROPE)), jnp.bfloat16),
+            pltpu.VMEM((2 * tok, LANES), jnp.float32),
             pltpu.VMEM((rows_all, WIDE), jnp.bfloat16),
             pltpu.VMEM((rows_all, keys_all), jnp.float32),
             pltpu.VMEM((ring, 2 * tok, heads * VH), jnp.bfloat16),
-            pltpu.SemaphoreType.DMA((4,)),
+            pltpu.SemaphoreType.DMA((2,)),
         ]
         + [each] * 6
         + [sems] * 8,
@@ -442,7 +455,7 @@
             collective_id=0, has_side_effects=True, vmem_limit_bytes=66 * 1000 * 1000
         ),
         name="attend",
-    )(queries, rows, w_key, w_value, turns)
+    )(prefix_len, queries, kv_new, kv_cache, kv_gain[None, :], w_key, w_value)
 
 
 def solution(mesh):

time: 158 us -> 154 us (0.975)
  other arithmetic: 5.51 us -> 0 us
  Pallas kernels: 146 us -> 148 us
    convert_element_type x5 -> x0, other arithmetic: 2.59 us -> none  [the longest x1 0.94 us: local(): latent = (raw * inv_rms * kv_gain[None, :]).astype(jnp.bfloat16)]
    pallas_call x1, Pallas kernels: 146 us -> 148 us  [local(): pl.pallas_call(functools.partial(kernel, (ring, tok, cache, heads)), out_...]
    concatenate x2 -> x0, other arithmetic: 1.63 us -> none  [the longest x1 1.51 us: local(): rows = jnp.concatenate([jnp.concatenate([kv_cache, bias], 1), new_rows], 0)]
where the time goes in v3:
time: 154 us; the launch traced here: 152 us
  Pallas kernels  148 us (96%)
  local copies, waits for them, and re-layouts  3.05 us (2%)
    pallas_call x1, Pallas kernels, local(): pl.pallas_call(functools.partial(kernel, (ring, tok, cache, heads)), out_...  148 us

profile of v3, /device:TPU:86, one launch (start us, length us, event | category | flops | bytes accessed | tf_op | source)
XLA Modules:
  0.0 151.8 jit_solution(242218680120576115)
XLA Ops:
  0.7 148.1 %attend.1 = bf16[64,16384]{1,0:T(8,128)(2,1)} custom-call(s32[1]{0:T(128)S(6)} %copy.9.start_ref, bf16[64,24576]{1,0:T(8,128)(2,1)} %q_hbm.1, bf16[64,576]{1,0:T(8,128)(2,1)} %new_ref.1, bf16[32,576]{1,0:T(8,128)(2,1)} %cache_ref.1, f32[1,512]{1,0:T(1,128)} %bitcast.1, bf16[512,512]{1,0:T(8,128)(2,1)} %wk_hbm.1, bf16[512,512]{1,0:T(8,128)(2,1)} %wv_hbm.1), custom_call_target="tpu_custom_call" | custom-call | tf_op jit(solution)/shard_map/attend/pallas_call | solution.py:429
  148.8 3.0 %copy.10 = bf16[64,16384]{1,0:T(8,128)(2,1)} copy(bf16[64,16384]{1,0:T(8,128)(2,1)} %attend.1) | data formatting | bytes 4194304

commit v4 on v3

--- a/solution.py
+++ b/solution.py
@@ -16,6 +16,7 @@
 WIDE = 640
 BLOCK = 1024
 LANES = 128
+PARTS = (0, 1, 2)
 AXES = ("gx", "px", "gy", "py", "z", "c")
 GROUPS = ("gx", "px", "gy", "py")
 SEQ = ("z", "c")
@@ -41,6 +42,7 @@
     turn_ref,
     qs,
     scores,
+    mixed,
     made,
     local_sem,
     ql_sem,
@@ -117,7 +119,7 @@
         slot = zz * 2 + core
         if part == 0:
             return keys.at[pl.ds(slot * cache, cache)]
-        return keys.at[pl.ds(cached_all + slot * tok, tok)]
+        return keys.at[pl.ds(cached_all + slot * tok + (part - 1) * (tok // 2), tok // 2)]
 
     def k_ring(way, d, part):
         ref = k_rows(far_slot(way, d), c, part)
@@ -188,7 +190,7 @@
     keys[cache_at, LATENT:] = jnp.concatenate([cache_ref[:, LATENT:], bias], 1)
 
     pl.semaphore_wait(barrier, 5)
-    for part in (0, 1):
+    for part in PARTS:
         k_ring(0, 0, part).start()
         k_ring(1, 0, part).start()
         k_core(0, 0, part).start()
@@ -205,11 +207,11 @@
     lax.fori_loop(0, units, q_start, 0)
 
     def k_step(d, carry):
-        for part in (0, 1):
+        for part in PARTS:
             for way in (0, 1):
                 k_ring_in(way, d, part).wait_recv()
 
-                @pl.when(jnp.logical_or(d < far - 1, part == way))
+                @pl.when(jnp.logical_or(d < far - 1, part % 2 == way))
                 def _():
                     k_ring(way, d, part).start()
 
@@ -232,9 +234,9 @@
     lax.fori_loop(1, far, k_step, 0)
     for way in (0, 1):
         w_ring(way, 1, 0).start()
-    for part in (0, 1):
-        k_ring_in(part, far, part).wait_recv()
-        k_core(part, far, part).start()
+    for part in PARTS:
+        k_ring_in(part % 2, far, part).wait_recv()
+        k_core(part % 2, far, part).start()
 
     def q_end(zz, carry):
         q_own(zz).wait()
@@ -247,7 +249,15 @@
     ones_lane = jnp.where(lane == 0, 1.0, 0.0).astype(jnp.bfloat16)
     scale = math.log2(math.e) / math.sqrt(NOPE + ROPE)
 
-    def unit(zz, turn, before_values):
+    def values(zz, turn):
+        for j in range(heads):
+            made[turn, :, j * VH : (j + 1) * VH] = jnp.dot(
+                mixed[j * chip : (j + 1) * chip, :],
+                w[zz, 1, :, j * VH : (j + 1) * VH],
+                preferred_element_type=jnp.float32,
+            ).astype(jnp.bfloat16)
+
+    def unit(zz):
         block = q[:, pl.ds(pl.multiple_of(zz * q_wide, LANES), q_wide)]
         for j in range(heads):
             at = j * (NOPE + ROPE)
@@ -293,14 +303,7 @@
             jnp.concatenate(parts, 1), keys[:, :LATENT], preferred_element_type=jnp.float32
         )
         norm = 1.0 / jnp.sum(total, axis=1, keepdims=True)
-        mixed = (acc * norm).astype(jnp.bfloat16)
-        before_values()
-        for j in range(heads):
-            made[turn, :, j * VH : (j + 1) * VH] = jnp.dot(
-                mixed[j * chip : (j + 1) * chip],
-                w[zz, 1, :, j * VH : (j + 1) * VH],
-                preferred_element_type=jnp.float32,
-            ).astype(jnp.bfloat16)
+        mixed[...] = (acc * norm).astype(jnp.bfloat16)
 
     def w_in(d, m):
         for way in (0, 1):
@@ -333,18 +336,18 @@
     def o_in(u):
         return copy(made.at[u, pl.ds(c * tok, tok)], o_into(u, 1 - c), o_s.at[u], o_r.at[u], mate)
 
-    for part in (0, 1):
+    for part in PARTS:
         k_core_in(0, 0, part).wait_recv()
 
     def k_rest(d, carry):
-        for part in (0, 1):
+        for part in PARTS:
             for way in (0, 1):
                 k_core_in(way, d, part).wait_recv()
         return carry
 
     lax.fori_loop(1, far, k_rest, 0)
-    for part in (0, 1):
-        k_core_in(part, far, part).wait_recv()
+    for part in PARTS:
+        k_core_in(part % 2, far, part).wait_recv()
 
     def step(u, carry):
         e = (u + 1) // 2
@@ -362,47 +365,63 @@
 
         @pl.when(u > 0)
         def _():
-            o_own(u - 1).start()
-            o_out(u - 1).start()
             w_side_in(1 - lax.rem(u, 2), e, 0).wait_recv()
 
-        def before_values():
-            way = 1 - lax.rem(u, 2) + (u + 1) // units
-
-            @pl.when(u > 0)
-            def _():
-                w_side_in(way, e, 1).wait_recv()
-
-        unit(chip_of(u), u, before_values)
-        return carry
-
+        @pl.when(u > 1)
+        def _():
+            o_own(u - 2).start()
+            o_out(u - 2).start()
+            values_in(u - 1)
+
+        before = u - 1 + (units - u) // units
+        values(chip_of(before), before)
+        unit(chip_of(u))
+        return carry
+
+    def values_in(u):
+        way = 1 - lax.rem(u, 2) + (u + 1) // units
+        w_side_in(way, (u + 1) // 2, 1).wait_recv()
+
+    mixed[...] = jnp.zeros_like(mixed)
     lax.fori_loop(0, units, step, 0)
-    o_own(units - 1).start()
-    o_out(units - 1).start()
-
-    for part in (0, 1):
+    o_own(units - 2).start()
+    o_out(units - 2).start()
+    values_in(units - 1)
+    values(chip_of(units - 1), units - 1)
+
+    for part in PARTS:
         k_core(0, 0, part).wait_send()
         for way in (0, 1):
             k_ring(way, 0, part).wait_send()
-            w_ring(way, 0, part).wait_send()
+    for m in (0, 1):
+        for way in (0, 1):
+            w_ring(way, 0, m).wait_send()
+    o_own(units - 1).start()
+    o_out(units - 1).start()
 
     def drain(d, carry):
-        for part in (0, 1):
-            for way in (0, 1):
-
-                @pl.when(jnp.logical_or(d < far - 1, part == way))
+        for way in (0, 1):
+            for part in PARTS:
+
+                @pl.when(jnp.logical_or(d < far - 1, part % 2 == way))
                 def _():
                     k_ring(way, d, part).wait_send()
-                    w_ring(way, d, part).wait_send()
 
                 k_core(way, d, part).wait_send()
-                w_side(way, d, part).wait_send()
+            for m in (0, 1):
+
+                @pl.when(jnp.logical_or(d < far - 1, m == way))
+                def _():
+                    w_ring(way, d, m).wait_send()
+
+                w_side(way, d, m).wait_send()
         return carry
 
     lax.fori_loop(1, far, drain, 0)
-    for part in (0, 1):
-        k_core(part, far, part).wait_send()
-        w_side(part, far, part).wait_send()
+    for part in PARTS:
+        k_core(part % 2, far, part).wait_send()
+    for m in (0, 1):
+        w_side(m, far, m).wait_send()
 
     def finish(u, carry):
         q_out(u).wait_send()
@@ -446,11 +465,13 @@
             pltpu.VMEM((2 * tok, LANES), jnp.float32),
             pltpu.VMEM((rows_all, WIDE), jnp.bfloat16),
             pltpu.VMEM((rows_all, keys_all), jnp.float32),
+            pltpu.VMEM((rows_all, LATENT), jnp.bfloat16),
             pltpu.VMEM((ring, 2 * tok, heads * VH), jnp.bfloat16),
             pltpu.SemaphoreType.DMA((2,)),
         ]
         + [each] * 6
-        + [sems] * 8,
+        + [pltpu.SemaphoreType.DMA((2, ring // 2 + 1, len(PARTS)))] * 4
+        + [sems] * 4,
         compiler_params=pltpu.CompilerParams(
             collective_id=0, has_side_effects=True, vmem_limit_bytes=66 * 1000 * 1000
         ),

time: 154 us -> 151 us (0.981)
  Pallas kernels: 148 us -> 144 us
    pallas_call x1, Pallas kernels: 148 us -> 144 us  [local(): pl.pallas_call(functools.partial(kernel, (ring, tok, cache, heads)), out_...]
where the time goes in v4:
time: 151 us; the launch traced here: 148 us
  Pallas kernels  144 us (95%)
  local copies, waits for them, and re-layouts  3.05 us (2%)
    pallas_call x1, Pallas kernels, local(): pl.pallas_call(functools.partial(kernel, (ring, tok, cache, heads)), out_...  144 us
    unnamed x1, local copies, waits for them, and re-layouts  3.05 us

profile of v4, /device:TPU:86, one launch (start us, length us, event | category | flops | bytes accessed | tf_op | source)
XLA Modules:
  0.0 148.1 jit_solution(6996508481652031865)
XLA Ops:
  0.7 144.4 %attend.1 = bf16[64,16384]{1,0:T(8,128)(2,1)} custom-call(s32[1]{0:T(128)S(6)} %copy.9.start_ref, bf16[64,24576]{1,0:T(8,128)(2,1)} %q_hbm.1, bf16[64,576]{1,0:T(8,128)(2,1)} %new_ref.1, bf16[32,576]{1,0:T(8,128)(2,1)} %cache_ref.1, f32[1,512]{1,0:T(1,128)} %bitcast.1, bf16[512,512]{1,0:T(8,128)(2,1)} %wk_hbm.1, bf16[512,512]{1,0:T(8,128)(2,1)} %wv_hbm.1), custom_call_target="tpu_custom_call" | custom-call | tf_op jit(solution)/shard_map/attend/pallas_call | solution.py:448
  145.0 3.0 %copy.10 = bf16[64,16384]{1,0:T(8,128)(2,1)} copy(bf16[64,16384]{1,0:T(8,128)(2,1)} %attend.1) | data formatting | bytes 4194304
